TPU v7x, 32 devices: a whole 2x2x4 slice. The times are simulated.
32 devices in a mesh: dp: 4 (over z), tensor: 8 (over y, x, core).
Axes of the slice: x: 2, y: 2, z: 4, core: 2. Of those that a mesh axis runs over, the one named last changes fastest.
Arguments:
- activations: bfloat16 [1024, 27648], P('dp', 'tensor'), may hold values from -6 to 6
- left_factor: float32 [216, 216], replicated, may hold values from -2 to 3, as said below
- right_factor: float32 [128, 128], replicated, may hold values from -2 to 3, as said below
- clip_scale: float32 [128, 216], replicated, may hold values from 0.5 to 3
- weight_rows: bfloat16 [27648, 5120], P('tensor'), may hold values from -0.0390625 to 0.0390625
- target: bfloat16 [1024, 5120], P('dp'), may hold values from -6 to 6
Outputs:
- grad_left: float32 [216, 216], replicated
- grad_right: float32 [128, 128], replicated
- grad_input: float32 [1024, 27648], P('dp', 'tensor')
Inputs may be any that keep to these rules, and one draw needn't show every extreme that they name: `left_factor`: the identity plus independent entries of order one over the square root of 216. `right_factor`: the identity plus independent entries of order one over the square root of 128.
All inputs are finite; a program needn't handle non-finite values.
Results may differ from a plain program's by a relative error of at most 0.007.
Values may be sent and summed in bfloat16 or wider, within the bound.
A program may use at most 128 MiB of HBM per device.

v0:
```python
import jax
import jax.numpy as jnp
from jax import lax
from jax.sharding import PartitionSpec as P


def local(activations, left_factor, right_factor, clip_scale, weight_rows, target):
    highest = lax.Precision.HIGHEST
    tok_rows = activations.shape[0]
    width_left = left_factor.shape[0]
    local_right = activations.shape[1] // width_left
    inputs = activations.reshape(tok_rows, local_right, width_left)
    moved = lax.all_to_all(inputs, "tensor", split_axis=0, concat_axis=1, tiled=True)
    mixed = jnp.einsum("tji,ik->tjk", moved.astype(jnp.float32), left_factor, precision=highest)
    rotated = jnp.einsum("jl,tjk->tlk", right_factor, mixed, precision=highest)
    bounded = jnp.tanh(rotated / clip_scale)
    clipped = (clip_scale * bounded).astype(jnp.bfloat16)
    clipped_back = lax.all_to_all(clipped, "tensor", split_axis=1, concat_axis=0, tiled=True)
    partial_out = jnp.dot(
        clipped_back.reshape(tok_rows, -1), weight_rows, preferred_element_type=jnp.float32
    )
    total = lax.psum(partial_out, "tensor")
    out_grad = (total - target.astype(jnp.float32)).astype(jnp.bfloat16)
    clipped_grad = lax.dot_general(
        out_grad, weight_rows, (((1,), (1,)), ((), ())), preferred_element_type=jnp.float32
    )
    clipped_grad = clipped_grad.reshape(tok_rows, local_right, width_left)
    grad_owned = lax.all_to_all(clipped_grad, "tensor", split_axis=0, concat_axis=1, tiled=True)
    rotated_grad = grad_owned * (1.0 - bounded * bounded)
    mixed_grad = jnp.einsum("jl,tlk->tjk", right_factor, rotated_grad, precision=highest)
    right_part = jnp.einsum("tjk,tlk->jl", mixed, rotated_grad, precision=highest)
    grad_back = lax.all_to_all(mixed_grad, "tensor", split_axis=1, concat_axis=0, tiled=True)
    input_grad = jnp.einsum("tjk,ik->tji", grad_back, left_factor, precision=highest).reshape(
        tok_rows, -1
    )
    left_part = jnp.einsum("tji,tjk->ik", inputs.astype(jnp.float32), grad_back, precision=highest)
    left_sum, right_sum = lax.psum((left_part, right_part), ("dp", "tensor"))
    return (left_sum, right_sum, input_grad)


def solution(mesh):
    placed = (P("dp", "tensor"), P(), P(), P(), P("tensor", None), P("dp", None))
    return jax.shard_map(
        local, mesh=mesh, in_specs=placed, out_specs=(P(), P(), P("dp", "tensor")), check_vma=False
    )
```

profile of v0, /device:TPU:8, one launch (start us, length us, event | category | flops | bytes accessed | tf_op | source)
XLA Modules:
  0.0 508.3 jit_solution(451690624203319944)
XLA Ops:
  7.2 0.0 copy-start
  7.2 0.0 all-reduce.4.cloned.1.call-start
  7.2 2.7 copy.31
  9.9 3.0 copy.32
  12.9 30.3 %all_to_all.69 = bf16[256,16,216]{2,1,0:T(8,128)(2,1)S(1)} all-to-all(bf16[256,16,216]{2,1,0:T(8,128)(2,1)} %copy.32), channel_id=1, replica_groups=mesh['dp'=4,'tensor'=8] {'tensor'}, dimensions={0} | all-to-all | bytes 3538944 | tf_op jit(solution)/shard_map/all_to_all | solution.py:13
  43.2 0.3 copy.33
  43.5 0.0 copy-start.2
  43.5 0.0 copy-start.3
  43.5 0.0 copy-done
  43.5 2.1 fusion.6
  45.7 0.0 copy-done.2
  45.7 0.0 copy-done.3
  45.7 0.0 copy-start.1
  45.7 4.7 multiply_convert_fusion
  50.4 0.0 copy-done.1
  50.4 4.5 copy.36
  54.9 30.1 %all_to_all.70 = bf16[32,128,216]{2,0,1:T(8,128)(2,1)S(1)} all-to-all(bf16[32,128,216]{2,0,1:T(8,128)(2,1)} %copy.36), channel_id=1, replica_groups=mesh['dp'=4,'tensor'=8] {'tensor'}, dimensions={1} | all-to-all | bytes 3538944 | tf_op jit(solution)/shard_map/all_to_all | solution.py:18
  85.0 2.6 copy.38
  87.6 5.2 %reshape.21 = bf16[256,3456]{1,0:T(8,128)(2,1)} reshape(bf16[8,32,16,216]{3,2,1,0:T(8,128)(2,1)} %copy.38) | data formatting | bytes 3538944 | tf_op jit(solution)/shard_map/reshape | solution.py:20
  92.8 18.0 %fusion.12 = f32[256,5120]{1,0:T(8,128)} fusion(bf16[256,3456]{1,0:T(8,128)(2,1)} %reshape.21, bf16[3456,5120]{1,0:T(8,128)(2,1)} %param.10), kind=kOutput, calls=%fused_computation.18 | convolution fusion | flops 9059696640 | bytes 42401792 | tf_op jit(solution)/shard_map/dot_general | solution.py:19
  110.8 0.0 all-reduce.4.cloned.1.call-update
  110.8 91.8 %all-reduce.4.cloned.1.call-done = f32[256,5120]{1,0:T(8,128)} async-done(((f32[256,5120]{1,0:T(8,128)}), f32[256,5120]{1,0:T(8,128)}) %all-reduce.4.cloned.1.call-update) | async-done | bytes 5242896 | tf_op jit(solution)/shard_map/psum | solution.py:22
  202.6 19.4 %fusion.1 = f32[256,3456]{0,1:T(8,128)} fusion(bf16[3456,5120]{1,0:T(8,128)(2,1)} %param.10, f32[256,5120]{1,0:T(8,128)} %all-reduce.4.cloned.1.call-done, bf16[256,5120]{1,0:T(8,128)(2,1)} %param.11), kind=kOutput, calls=%fused_computation.5 | convolution fusion | flops 9063628800 | bytes 46792704 | tf_op jit(solution)/shard_map/dot_general | solution.py:24
  222.0 5.3 %copy.40 = f32[256,16,216]{2,1,0:T(8,128)} copy(f32[256,16,216]{0,2,1:T(8,128)} %bitcast.63) | data formatting | bytes 7077888 | tf_op jit(solution)/shard_map/reshape | solution.py:27
  227.3 52.6 %all_to_all.71 = f32[256,16,216]{2,1,0:T(8,128)S(1)} all-to-all(f32[256,16,216]{2,1,0:T(8,128)} %copy.40), channel_id=1, replica_groups=mesh['dp'=4,'tensor'=8] {'tensor'}, dimensions={0} | all-to-all | bytes 7077888 | tf_op jit(solution)/shard_map/all_to_all | solution.py:28
  279.9 2.7 copy.41
  282.6 5.5 %copy.42 = f32[32,128,216]{1,2,0:T(8,128)} copy(f32[32,128,216]{2,1,0:T(8,128)} %bitcast.55) | data formatting | bytes 7077888 | tf_op jit(solution)/shard_map/all_to_all | solution.py:28
  288.1 6.4 %convolution_bitcast_fusion = f32[32,128,216]{1,2,0:T(8,128)} fusion(f32[32,128,216]{1,2,0:T(8,128)} %copy.42, f32[32,128,216]{1,2,0:T(8,128)} %get-tuple-element.15, f32[128,128]{1,0:T(8,128)S(1)} %copy-done.2), kind=kOutput, calls=%fused_computation.6 | convolution fusion | flops 1361608704 | bytes 10682368 | tf_op jit(solution)/shard_map/jl,tlk->tjk/dot_general | solution.py:30
  294.5 5.3 %copy.43 = f32[32,128,216]{2,0,1:T(8,128)} copy(f32[32,128,216]{1,2,0:T(8,128)} %convolution_bitcast_fusion) | data formatting | bytes 7077888 | tf_op jit(solution)/shard_map/jl,tlk->tjk/transpose | solution.py:30
  299.7 4.6 all-to-all-start.3
  304.3 0.3 all-reduce.6.cloned.1.call-start
  304.5 10.7 %fusion.3 = f32[128,128]{1,0:T(8,128)} fusion(f32[32,128,216]{1,2,0:T(8,128)} %copy-done.1, f32[32,128,216]{1,2,0:T(8,128)} %copy.42, f32[32,128,216]{1,2,0:T(8,128)} %get-tuple-element.15), kind=kOutput, calls=%fused_computation.9 | convolution fusion | flops 1361608704 | bytes 10682368 | tf_op jit(solution)/shard_map/tjk,tlk->jl/dot_general | solution.py:31
  315.3 38.1 %all-to-all-done.3 = f32[32,128,216]{2,0,1:T(8,128)} async-done(((f32[32,128,216]{2,0,1:T(8,128)}), f32[32,128,216]{2,0,1:T(8,128)}, u32[]{:S(2)}, u32[]{:S(2)}) %all-to-all-start.3) | async-done | bytes 3538976 | tf_op jit(solution)/shard_map/all_to_all | solution.py:32
  353.4 6.5 %copy.45 = f32[8,32,16,216]{3,2,1,0:T(8,128)} copy(f32[8,32,16,216]{3,1,2,0:T(8,128)} %bitcast.17) | data formatting | bytes 7077888 | tf_op jit(solution)/shard_map/all_to_all | solution.py:32
  359.9 5.1 %copy.46 = f32[256,16,216]{0,2,1:T(8,128)} copy(f32[256,16,216]{2,1,0:T(8,128)} %bitcast.56) | data formatting | bytes 7077888 | tf_op jit(solution)/shard_map/all_to_all | solution.py:32
  365.0 4.6 convolution_bitcast_fusion.1
  369.6 0.0 all-reduce.6.cloned.1.call-update
  369.6 7.1 %fusion.4 = f32[256,16,216]{0,2,1:T(8,128)} fusion(f32[256,16,216]{0,2,1:T(8,128)} %copy.46, f32[216,216]{1,0:T(8,128)S(1)} %copy-done), kind=kOutput, calls=%fused_computation.10 | convolution fusion | flops 2293235712 | bytes 7264512 | tf_op jit(solution)/shard_map/tjk,ik->tji/dot_general | solution.py:33
  376.7 5.2 %copy.49 = f32[256,3456]{1,0:T(8,128)} copy(f32[256,3456]{0,1:T(8,128)} %bitcast.59) | data formatting | bytes 7077888
  381.9 116.3 %all-reduce.6.cloned.1.call-done = (f32[216,216]{0,1:T(8,128)}, f32[128,128]{1,0:T(8,128)}) async-done(((f32[216,216]{0,1:T(8,128)}, f32[128,128]{1,0:T(8,128)}), (f32[216,216]{0,1:T(8,128)}, f32[128,128]{1,0:T(8,128)})) %all-reduce.6.cloned.1.call-update) | async-done | bytes 252176 | tf_op jit(solution)/shard_map/psum | solution.py:37
  498.2 1.7 copy.48
  499.9 1.5 copy.59
Async XLA Ops:
  7.2 36.4 %copy-start = (f32[216,216]{1,0:T(8,128)S(1)}, f32[216,216]{1,0:T(8,128)}, u32[]{:S(2)}) copy-start(f32[216,216]{1,0:T(8,128)} %param.7) | copy-start | bytes 559876
  7.2 195.4 %all-reduce.4.cloned.1.call-start = ((), (), s32[]{:S(2)}) async-start(), calls=%async_computation.4 | async-start | bytes 10485760 | tf_op jit(solution)/shard_map/psum | solution.py:22
  43.5 2.2 copy-start.2
  43.5 2.2 copy-start.3
  45.7 4.7 copy-start.1
  299.7 53.7 %all-to-all-start.3 = ((f32[32,128,216]{2,0,1:T(8,128)}), f32[32,128,216]{2,0,1:T(8,128)}, u32[]{:S(2)}, u32[]{:S(2)}) async-start(f32[32,128,216]{2,0,1:T(8,128)} %copy.43), calls=%async_computation.3 | async-start | bytes 8388608 | tf_op jit(solution)/shard_map/all_to_all | solution.py:32
  304.3 193.9 %all-reduce.6.cloned.1.call-start = ((), (), s32[]{:S(2)}) async-start(), calls=%async_computation.5 | async-start | bytes 573440 | tf_op jit(solution)/shard_map/psum | solution.py:37
Sparse Core Ops, SparseCore 0:
  110.9 91.6 all-reduce.3
  369.7 128.4 all-reduce.5
where the time goes:
time: 510 us; the launch traced here: 508 us
  waiting for transfers between devices  246 us (48%)
  blocking collectives  113 us (22%)
  matrix products  72.9 us (14%)
  local copies, waits for them, and re-layouts  57 us (11%)
  between operations  14.1 us (3%)
    psum x1, waiting for transfers between devices, local(): left_sum, right_sum = lax.psum((left_part, right_part), ('dp', 'tensor'))  116 us
    psum x1, waiting for transfers between devices, local(): total = lax.psum(partial_out, 'tensor')  91.8 us
    all_to_all x1, blocking collectives, local(): lax.all_to_all(clipped_grad, 'tensor', split_axis=0, concat_axis=1, tiled...  52.6 us
    all_to_all x1, waiting for transfers between devices, local(): lax.all_to_all(mixed_grad, 'tensor', split_axis=1, concat_axis=0, tiled=T...  38.1 us
    all_to_all x1, blocking collectives, local(): lax.all_to_all(inputs, 'tensor', split_axis=0, concat_axis=1, tiled=True)  30.3 us
    all_to_all x1, blocking collectives, local(): lax.all_to_all(clipped, 'tensor', split_axis=1, concat_axis=0, tiled=True)  30.1 us
    dot_general x1, matrix products, local(): lax.dot_general(out_grad, weight_rows, (((1,), (1,)), ((), ())), preferre...  19.4 us
    dot_general x1, matrix products, local(): jnp.dot(clipped_back.reshape(tok_rows, -1), weight_rows, preferred_elemen...  18 us
  transfers between devices with their start and end apart: 3, of which 3 were waited for; matrix products, arithmetic and copies ran while one was open for 5% of the time, Pallas kernels for 0%

commit v1 on v0

--- a/solution.py
+++ b/solution.py
@@ -19,7 +19,9 @@
     partial_out = jnp.dot(
         clipped_back.reshape(tok_rows, -1), weight_rows, preferred_element_type=jnp.float32
     )
-    total = lax.psum(partial_out, "tensor")
+    total = partial_out
+    for hop in (1, 2, 4):
+        total = total + lax.ppermute(total, "tensor", [(dev, dev ^ hop) for dev in range(8)])
     out_grad = (total - target.astype(jnp.float32)).astype(jnp.bfloat16)
     clipped_grad = lax.dot_general(
         out_grad, weight_rows, (((1,), (1,)), ((), ())), preferred_element_type=jnp.float32

time: 510 us -> 656 us (1.29)
  waiting for transfers between devices: 246 us -> 392 us
    ppermute x0 -> x3, waiting for transfers between devices: none -> 237 us  [local(): lax.ppermute(total, 'tensor', [(dev, dev ^ hop) for dev in range(8)])]
    psum x1 -> x0, waiting for transfers between devices: 91.8 us -> none  [local(): total = lax.psum(partial_out, 'tensor')]
  transfers between devices with their start and end apart: 3 -> 5, of which waited for: 3 -> 5; matrix products, arithmetic and copies ran while one was open for 5% -> 4% of each run, Pallas kernels for 0% -> 0%
where the time goes in v1:
time: 656 us; the launch traced here: 655 us
  waiting for transfers between devices  392 us (60%)
  blocking collectives  113 us (17%)
  matrix products  71.7 us (11%)
  local copies, waits for them, and re-layouts  56.9 us (9%)
  between operations  14.1 us (2%)
    ppermute x3, waiting for transfers between devices, local(): lax.ppermute(total, 'tensor', [(dev, dev ^ hop) for dev in range(8)])  237 us
    psum x1, waiting for transfers between devices, local(): left_sum, right_sum = lax.psum((left_part, right_part), ('dp', 'tensor'))  116 us
    all_to_all x1, blocking collectives, local(): lax.all_to_all(clipped_grad, 'tensor', split_axis=0, concat_axis=1, tiled...  52.6 us
    all_to_all x1, waiting for transfers between devices, local(): lax.all_to_all(mixed_grad, 'tensor', split_axis=1, concat_axis=0, tiled=T...  38.3 us
    all_to_all x1, blocking collectives, local(): lax.all_to_all(inputs, 'tensor', split_axis=0, concat_axis=1, tiled=True)  30.3 us
    all_to_all x1, blocking collectives, local(): lax.all_to_all(clipped, 'tensor', split_axis=1, concat_axis=0, tiled=True)  30.1 us
    dot_general x1, matrix products, local(): lax.dot_general(out_grad, weight_rows, (((1,), (1,)), ((), ())), preferre...  19.7 us
    dot_general x1, matrix products, local(): jnp.dot(clipped_back.reshape(tok_rows, -1), weight_rows, preferred_elemen...  16.5 us
  transfers between devices with their start and end apart: 5, of which 5 were waited for; matrix products, arithmetic and copies ran while one was open for 4% of the time, Pallas kernels for 0%

profile of v1, /device:TPU:8, one launch (start us, length us, event | category | flops | bytes accessed | tf_op | source)
XLA Modules:
  0.0 654.9 jit_solution(13717384632485683311)
XLA Ops:
  7.2 0.0 copy-start
  7.2 2.7 copy.31
  9.9 3.0 copy.32
  12.9 30.3 %all_to_all.69 = bf16[256,16,216]{2,1,0:T(8,128)(2,1)S(1)} all-to-all(bf16[256,16,216]{2,1,0:T(8,128)(2,1)} %copy.32), channel_id=1, replica_groups=mesh['dp'=4,'tensor'=8] {'tensor'}, dimensions={0} | all-to-all | bytes 3538944 | tf_op jit(solution)/shard_map/all_to_all | solution.py:13
  43.2 0.3 copy.33
  43.4 0.0 copy-start.2
  43.4 0.0 copy-start.3
  43.5 0.0 copy-done
  43.5 2.1 fusion.6
  45.6 0.0 copy-done.2
  45.6 0.0 copy-done.3
  45.6 0.0 copy-start.1
  45.6 4.7 multiply_convert_fusion
  50.3 0.0 copy-done.1
  50.3 4.5 copy.36
  54.9 30.1 %all_to_all.70 = bf16[32,128,216]{2,0,1:T(8,128)(2,1)S(1)} all-to-all(bf16[32,128,216]{2,0,1:T(8,128)(2,1)} %copy.36), channel_id=1, replica_groups=mesh['dp'=4,'tensor'=8] {'tensor'}, dimensions={1} | all-to-all | bytes 3538944 | tf_op jit(solution)/shard_map/all_to_all | solution.py:18
  84.9 2.6 copy.38
  87.5 5.1 reshape.21
  92.7 16.5 %fusion.12 = f32[256,5120]{1,0:T(8,128)S(1)} fusion(bf16[256,3456]{1,0:T(8,128)(2,1)} %reshape.21, bf16[3456,5120]{1,0:T(8,128)(2,1)} %param.10), kind=kOutput, calls=%fused_computation.18 | convolution fusion | flops 9059696640 | bytes 42401792 | tf_op jit(solution)/shard_map/dot_general | solution.py:19
  109.2 0.1 collective-permute-start
  109.2 8.6 %collective-permute-done = f32[256,5120]{1,0:T(8,128)S(1)} collective-permute-done((f32[256,5120]{1,0:T(8,128)S(1)}, f32[256,5120]{1,0:T(8,128)S(1)}, u32[]{:S(2)}, u32[]{:S(2)}) %collective-permute-start) | collective-permute-done | bytes 5242912 | tf_op jit(solution)/shard_map/ppermute | solution.py:24
  117.9 0.8 add.13
  118.7 0.6 collective-permute-start.1
  119.4 114.5 %collective-permute-done.1 = f32[256,5120]{1,0:T(8,128)S(1)} collective-permute-done((f32[256,5120]{1,0:T(8,128)S(1)}, f32[256,5120]{1,0:T(8,128)S(1)}, u32[]{:S(2)}, u32[]{:S(2)}) %collective-permute-start.1) | collective-permute-done | bytes 5242912 | tf_op jit(solution)/shard_map/ppermute | solution.py:24
  233.9 0.6 add.14
  234.5 0.6 collective-permute-start.2
  235.1 113.8 %collective-permute-done.2 = f32[256,5120]{1,0:T(8,128)} collective-permute-done((f32[256,5120]{1,0:T(8,128)S(1)}, f32[256,5120]{1,0:T(8,128)}, u32[]{:S(2)}, u32[]{:S(2)}) %collective-permute-start.2) | collective-permute-done | bytes 5242912 | tf_op jit(solution)/shard_map/ppermute | solution.py:24
  348.9 19.7 %fusion.1 = f32[256,3456]{0,1:T(8,128)} fusion(bf16[3456,5120]{1,0:T(8,128)(2,1)} %param.10, bf16[256,5120]{1,0:T(8,128)(2,1)} %param.11, f32[256,5120]{1,0:T(8,128)S(1)} %add.14, f32[256,5120]{1,0:T(8,128)} %collective-permute-done.2), kind=kOutput, calls=%fused_computation.5 | convolution fusion | flops 9064939520 | bytes 52035584 | tf_op jit(solution)/shard_map/dot_general | solution.py:26
  368.6 5.3 copy.40
  373.9 52.6 %all_to_all.71 = f32[256,16,216]{2,1,0:T(8,128)S(1)} all-to-all(f32[256,16,216]{2,1,0:T(8,128)} %copy.40), channel_id=1, replica_groups=mesh['dp'=4,'tensor'=8] {'tensor'}, dimensions={0} | all-to-all | bytes 7077888 | tf_op jit(solution)/shard_map/all_to_all | solution.py:30
  426.5 2.6 copy.41
  429.1 5.4 copy.42
  434.6 6.3 convolution_bitcast_fusion
  440.9 5.2 copy.43
  446.1 4.6 all-to-all-start.3
  450.7 0.0 all-reduce.3.cloned.1.call-start
  450.8 10.7 %fusion.3 = f32[128,128]{1,0:T(8,128)} fusion(f32[32,128,216]{1,2,0:T(8,128)} %copy-done.1, f32[32,128,216]{1,2,0:T(8,128)} %copy.42, f32[32,128,216]{1,2,0:T(8,128)} %get-tuple-element.15), kind=kOutput, calls=%fused_computation.9 | convolution fusion | flops 1361608704 | bytes 10682368 | tf_op jit(solution)/shard_map/tjk,tlk->jl/dot_general | solution.py:33
  461.5 38.3 %all-to-all-done.3 = f32[32,128,216]{2,0,1:T(8,128)} async-done(((f32[32,128,216]{2,0,1:T(8,128)}), f32[32,128,216]{2,0,1:T(8,128)}, u32[]{:S(2)}, u32[]{:S(2)}) %all-to-all-start.3) | async-done | bytes 3538976 | tf_op jit(solution)/shard_map/all_to_all | solution.py:34
  499.8 6.6 %copy.45 = f32[8,32,16,216]{3,2,1,0:T(8,128)} copy(f32[8,32,16,216]{3,1,2,0:T(8,128)} %bitcast.17) | data formatting | bytes 7077888 | tf_op jit(solution)/shard_map/all_to_all | solution.py:34
  506.4 5.1 copy.46
  511.5 4.6 convolution_bitcast_fusion.1
  516.0 0.0 all-reduce.3.cloned.1.call-update
  516.1 7.1 %fusion.4 = f32[256,16,216]{0,2,1:T(8,128)} fusion(f32[256,16,216]{0,2,1:T(8,128)} %copy.46, f32[216,216]{1,0:T(8,128)S(1)} %copy-done), kind=kOutput, calls=%fused_computation.10 | convolution fusion | flops 2293235712 | bytes 7264512 | tf_op jit(solution)/shard_map/tjk,ik->tji/dot_general | solution.py:35
  523.2 5.2 copy.49
  528.3 116.5 %all-reduce.3.cloned.1.call-done = (f32[216,216]{0,1:T(8,128)}, f32[128,128]{1,0:T(8,128)}) async-done(((f32[216,216]{0,1:T(8,128)}, f32[128,128]{1,0:T(8,128)}), (f32[216,216]{0,1:T(8,128)}, f32[128,128]{1,0:T(8,128)})) %all-reduce.3.cloned.1.call-update) | async-done | bytes 252176 | tf_op jit(solution)/shard_map/psum | solution.py:39
  644.8 1.7 copy.48
  646.6 1.5 copy.58
Async XLA Ops:
  7.2 36.3 %copy-start = (f32[216,216]{1,0:T(8,128)S(1)}, f32[216,216]{1,0:T(8,128)}, u32[]{:S(2)}) copy-start(f32[216,216]{1,0:T(8,128)} %param.7) | copy-start | bytes 559876
  43.4 2.2 copy-start.2
  43.4 2.2 copy-start.3
  45.6 4.7 copy-start.1
  109.2 8.7 %collective-permute-start = (f32[256,5120]{1,0:T(8,128)S(1)}, f32[256,5120]{1,0:T(8,128)S(1)}, u32[]{:S(2)}, u32[]{:S(2)}) collective-permute-start(f32[256,5120]{1,0:T(8,128)S(1)} %fusion.12), channel_id=1, source_target_pairs={{0,1},{1,0},{2,3},{3,2},{4,5},{5,4},{6,7},{7,6},{8,9},{9,8},{10,11... | collective-permute-start | bytes 15728648 | tf_op jit(solution)/shard_map/ppermute | solution.py:24
  118.7 115.1 %collective-permute-start.1 = (f32[256,5120]{1,0:T(8,128)S(1)}, f32[256,5120]{1,0:T(8,128)S(1)}, u32[]{:S(2)}, u32[]{:S(2)}) collective-permute-start(f32[256,5120]{1,0:T(8,128)S(1)} %add.13), channel_id=1, source_target_pairs={{0,2},{1,3},{2,0},{3,1},{4,6},{5,7},{6,4},{7,5},{8,10},{9,11},{10,... | collective-permute-start | bytes 15728648 | tf_op jit(solution)/shard_map/ppermute | solution.py:24
  234.5 114.4 %collective-permute-start.2 = (f32[256,5120]{1,0:T(8,128)S(1)}, f32[256,5120]{1,0:T(8,128)}, u32[]{:S(2)}, u32[]{:S(2)}) collective-permute-start(f32[256,5120]{1,0:T(8,128)S(1)} %add.14), channel_id=1, source_target_pairs={{0,4},{1,5},{2,6},{3,7},{4,0},{5,1},{6,2},{7,3},{8,12},{9,13},{10,... | collective-permute-start | bytes 15728648 | tf_op jit(solution)/shard_map/ppermute | solution.py:24
  446.1 53.7 %all-to-all-start.3 = ((f32[32,128,216]{2,0,1:T(8,128)}), f32[32,128,216]{2,0,1:T(8,128)}, u32[]{:S(2)}, u32[]{:S(2)}) async-start(f32[32,128,216]{2,0,1:T(8,128)} %copy.43), calls=%async_computation.3 | async-start | bytes 8388608 | tf_op jit(solution)/shard_map/all_to_all | solution.py:34
  450.7 194.1 %all-reduce.3.cloned.1.call-start = ((), (), s32[]{:S(2)}) async-start(), calls=%async_computation.4 | async-start | bytes 573440 | tf_op jit(solution)/shard_map/psum | solution.py:39
Sparse Core Ops, SparseCore 0:
  516.2 128.5 all-reduce.2
